TPU v7x, 256 devices: a whole 4x4x8 slice. The times are simulated.
256 devices in a mesh: ctx: 128 (over x, y_hi, z, core), head: 2 (over y_lo).
Axes of the slice: x: 4, y: 4 (y_hi: 2, y_lo: 2; y = y_hi * 2 + y_lo), z: 8, core: 2. Of those that a mesh axis runs over, the one named last changes fastest.
Arguments:
- queries: bfloat16 [16384, 2048], P('ctx', 'head'), may hold values from -160 to 160
- rotated_keys: bfloat16 [16384, 512], P('ctx', 'head'), may hold values from -6 to 6
- value_matrix: bfloat16 [16384, 512], P('ctx', 'head'), may hold values from -6 to 6
- doc_lengths: int32 [8], replicated, may hold values from 1 to 12288, 16384 in all
- scored: int32 [512], P('ctx'), may hold values from 0 to 127, as said below
- residual: bfloat16 [512, 4096], P('ctx', 'head'), may hold values from -18 to 18
- norm_gain: float32 [4096], P('head'), may hold values from 0.5 to 1.5
- out_weight: bfloat16 [2048, 4096], P('head'), may hold values from -0.5 to 0.5
- lm_weight: bfloat16 [4096, 128256], P('head', 'ctx'), may hold values from -0.40625 to 0.40625
- token_ids: int32 [512], replicated, may hold values from 0 to 128255
- old_logp: float32 [512], replicated, may hold values from -24 to -9
- advantage: float32 [512], replicated, may hold values from -3 to 3
Outputs:
- attended: bfloat16 [16384, 2048], P('ctx', 'head')
- log_probs: float32 [512], replicated
- token_loss: float32 [512], replicated
Inputs may be any that keep to these rules, and one draw needn't show every extreme that they name: `scored`: each aligned block of 4 entries holds distinct increasing offsets. `doc_lengths`: the longest document has exactly three quarters of 16384 positions.
All inputs are finite; a program needn't handle non-finite values.
Results may differ from a plain program's by a relative error of at most 0.0065.
Values may be sent and summed in bfloat16 or wider, within the bound.
No kernel may reach another device: no remote copies, remote signals or barrier semaphores. Data moves between devices by JAX's collectives and lax.ppermute only.
A program may use at most 128 MiB of HBM per device.

v0:
```python
import math

import jax
import jax.numpy as jnp
from jax import lax
from jax.sharding import Mesh
from jax.sharding import PartitionSpec as P

HEAD_SIZE = 128
CTX = ("ctx_0", "ctx_1", "ctx_2", "ctx_3")
CTX_HEAD = ("ctx_0", "ctx_1", "ctx_2", "ctx_3", "head")


masked_score = -1e30


def side_by_side(arrays, axis, dim, along):
    both = jnp.concatenate(arrays, axis=along)
    whole, at, outs = (lax.all_gather(both, axis, axis=dim, tiled=True), 0, [])
    for a in arrays:
        outs.append(lax.slice_in_dim(whole, at, at + a.shape[along], axis=along))
        at += a.shape[along]
    return tuple(outs)


def in_blocks(shard, dim, peers):
    before, after = (shard.shape[:dim], shard.shape[dim + 1 :])
    return jnp.moveaxis(shard.reshape(*before, peers, -1, *after), dim, 0)


def sum_at_owner(shard, axis, dim):
    pieces = in_blocks(shard, dim, lax.axis_size(axis))
    arrived = lax.all_to_all(pieces, axis, split_axis=0, concat_axis=0, tiled=True)
    return arrived.astype(jnp.float32).sum(axis=0)


def sent_to_all(shard, axis):
    peers = lax.axis_size(axis)
    return lax.all_to_all(
        jnp.broadcast_to(shard[None], (peers, *shard.shape)), axis, 0, 0, tiled=True
    )


def of_everyone(shard, axis):
    everything = sent_to_all(shard, axis)
    return jnp.sum(everything, axis=0)


def all_in_one(shard, axis):
    leaves = jax.tree.leaves(shard)
    order = sorted(range(len(leaves)), key=lambda k: -leaves[k].size)
    width = (1, *leaves[order[0]].shape)[-1]
    lines = [
        jnp.pad(leaves[k].reshape(-1), (0, -leaves[k].size % width)).reshape(-1, width)
        for k in order
    ]
    both, at, found = (lax.all_gather(jnp.concatenate(lines), axis), 0, {})
    for k, line in zip(order, lines):
        slab = both[:, at : at + len(line)].reshape(len(both), -1)
        found[k] = slab[:, : leaves[k].size].reshape(-1, *leaves[k].shape)
        at += len(line)
    numbers = iter(range(len(leaves)))
    return jax.tree.map(lambda _: found[next(numbers)], shard)


def merged_by_axis(shard, axes, combine):
    for axis in axes:
        pieces = all_in_one(shard, axis)
        shard = jax.tree.map(lambda part: part[0], pieces)
        for k in range(1, lax.axis_size(axis)):
            shard = combine(shard, jax.tree.map(lambda part: part[k], pieces))
    return shard


def doc_index(positions, doc_ends):
    return jnp.sum((positions[:, None] >= doc_ends[None, :]).astype(jnp.int32), axis=1)


def attend_rows(running, context, key_part, value_part, offset):
    query_heads, query_pos, query_doc, doc_ends, first_start, skipping = context
    row_top, row_total, accumulated = running
    row_count = key_part.shape[0]
    kv_heads = query_heads.shape[1]
    key_head_rows = key_part.reshape(row_count, kv_heads, HEAD_SIZE)
    value_head_rows = value_part.reshape(row_count, kv_heads, HEAD_SIZE)
    scores = jnp.einsum(
        "qkgd,rkd->kgqr", query_heads, key_head_rows, preferred_element_type=jnp.float32
    ) * HEAD_SIZE ** (-0.5)
    key_pos = offset + jnp.arange(row_count, dtype=jnp.int32)
    allowed = (
        (key_pos[None, :] <= query_pos[:, None])
        & (key_pos[None, :] >= 0)
        & (doc_index(key_pos, doc_ends)[None, :] == query_doc[:, None])
    )
    scores = jnp.where(allowed, scores, masked_score)
    new_top = jnp.maximum(row_top, jnp.max(scores, axis=-1))
    weights = jnp.where(allowed, jnp.exp(scores - new_top[..., None]), 0.0)
    rescale = jnp.exp(row_top - new_top)
    row_total = row_total * rescale + jnp.sum(weights, axis=-1)
    update = jnp.einsum(
        "kgqr,rkd->kgqd",
        weights.astype(jnp.bfloat16),
        value_head_rows,
        preferred_element_type=jnp.float32,
    )
    accumulated = accumulated * rescale[..., None] + update
    return (new_top, row_total, accumulated)


def attend_piece(running, shard_piece, context):
    key_rows, value_rows = shard_piece
    row_count = key_rows.shape[0]
    block_rows = math.gcd(row_count, 512)
    block_count = row_count // block_rows

    def one_block(block_index, carried):
        start_row = block_index * block_rows
        key_part = lax.dynamic_slice_in_dim(key_rows, start_row, block_rows, 0)
        value_part = lax.dynamic_slice_in_dim(value_rows, start_row, block_rows, 0)
        return attend_rows(carried, context, key_part, value_part, start_row)

    return lax.fori_loop(0, block_count, one_block, running)


def combine(earlier, later):
    top_one, sum_one, target_one = earlier
    top_two, sum_two, target_two = later
    new_top = jnp.maximum(top_one, top_two)
    merged_sum = sum_one * jnp.exp(top_one - new_top) + sum_two * jnp.exp(top_two - new_top)
    return (new_top, merged_sum, target_one + target_two)


def per_device(
    queries,
    rotated_keys,
    value_matrix,
    doc_lengths,
    scored,
    residual,
    norm_gain,
    out_weight,
    lm_weight,
    token_ids,
    old_logp,
    advantage,
):
    tok_rows = queries.shape[0]
    kv_heads = rotated_keys.shape[1] // HEAD_SIZE
    group_count = queries.shape[1] // rotated_keys.shape[1]
    my_index = lax.axis_index(CTX)
    doc_ends = jnp.cumsum(doc_lengths)
    doc_starts = doc_ends - doc_lengths
    query_pos = my_index * tok_rows + jnp.arange(tok_rows, dtype=jnp.int32)
    query_doc = doc_index(query_pos, doc_ends)
    first_start = jnp.max(jnp.where(doc_starts <= query_pos[0], doc_starts, 0))
    query_heads = queries.reshape(tok_rows, kv_heads, group_count, HEAD_SIZE)
    context = (query_heads, query_pos, query_doc, doc_ends, first_start, False)
    state_shape = (kv_heads, group_count, tok_rows)
    initial = (
        jnp.full(state_shape, masked_score, jnp.float32),
        jnp.zeros(state_shape, jnp.float32),
        jnp.zeros(state_shape + (HEAD_SIZE,), jnp.float32),
    )
    row_top, row_total, accumulated = attend_piece(
        initial, side_by_side((rotated_keys, value_matrix), CTX, 0, 1), context
    )
    result = accumulated / row_total[..., None]
    attended = (
        jnp.transpose(result, (2, 0, 1, 3))
        .reshape(tok_rows, kv_heads * group_count * HEAD_SIZE)
        .astype(jnp.bfloat16)
    )
    chosen = jnp.take(attended, scored, axis=0)
    partial_value = jnp.dot(chosen, out_weight, preferred_element_type=jnp.float32)
    projected = sum_at_owner(partial_value.astype(jnp.bfloat16), "head", 1)
    hidden = residual.astype(jnp.float32) + projected
    squares = of_everyone(jnp.sum(hidden * hidden, axis=1), "head")
    full_width = hidden.shape[1] * lax.axis_size("head")
    normed = (
        hidden * lax.rsqrt(squares[:, None] / full_width + 1e-05) * norm_gain[None, :]
    ).astype(jnp.bfloat16)
    partial_logits = jnp.dot(
        lax.all_gather(normed, CTX, axis=0, tiled=True),
        lm_weight,
        preferred_element_type=jnp.float32,
    )
    logits = sum_at_owner(partial_logits.astype(jnp.bfloat16), "head", 1)
    vocab_rows = logits.shape[1]
    vocab_start = (
        my_index * vocab_rows * lax.axis_size("head") + lax.axis_index("head") * vocab_rows
    )
    local_ids = token_ids - vocab_start
    matches = local_ids[:, None] == jnp.arange(vocab_rows, dtype=jnp.int32)[None, :]
    target_part = jnp.sum(jnp.where(matches, logits, 0.0), axis=1)
    local_top = jnp.max(logits, axis=1)
    sum_part = jnp.sum(jnp.exp(logits - local_top[:, None]), axis=1)
    global_top, exp_total, target = merged_by_axis(
        (local_top, sum_part, target_part), CTX_HEAD, combine
    )
    log_probs = target - global_top - jnp.log(exp_total)
    ratio = jnp.exp(jnp.clip(log_probs - old_logp, -4.0, 4.0))
    token_loss = -jnp.minimum(ratio * advantage, jnp.clip(ratio, 0.8, 1.2) * advantage)
    return (attended, log_probs, token_loss)


def solution(mesh):
    finer = Mesh(
        mesh.devices.reshape(4, 2, 8, 2, mesh.shape["head"]),
        ("ctx_0", "ctx_1", "ctx_2", "ctx_3", "head"),
    )
    placed = (
        P(CTX, "head"),
        P(CTX, "head"),
        P(CTX, "head"),
        P(),
        P(CTX),
        P(CTX, "head"),
        P("head"),
        P("head", None),
        P("head", CTX),
        P(),
        P(),
        P(),
    )
    return jax.shard_map(
        per_device,
        mesh=finer,
        in_specs=placed,
        out_specs=(P(CTX, "head"), P(), P()),
        check_vma=False,
    )
```

profile of v0, /device:TPU:1, one launch (start us, length us, event | category | flops | bytes accessed | tf_op | source)
XLA Modules:
  0.0 491.9 jit_solution(17511669347726125021)
XLA Ops:
  10.7 1.1 copy.48
  13.5 137.7 %all-gather.14.cloned.1.call-done = bf16[16384,512]{0,1:T(8,128)(2,1)} async-done(((bf16[128,512]{0,1:T(8,128)(2,1)}), bf16[16384,512]{0,1:T(8,128)(2,1)}) %all-gather.14.cloned.1.call-update) | async-done | bytes 16777232 | tf_op jit(solution)/shard_map/all_gather | solution.py:19
  151.2 11.4 %fusion.76 = (bf16[16384,256]{0,1:T(8,128)(2,1)}, bf16[16384,256]{0,1:T(8,128)(2,1)}) fusion(bf16[16384,512]{0,1:T(8,128)(2,1)} %all-gather.14.cloned.1.call-done), kind=kLoop, calls=%fused_computation.157 | loop fusion | bytes 33554432 | tf_op jit(solution)/shard_map/slice | solution.py:21
  162.7 113.7 %while.18 = (s32[]{:T(128)}, f32[2,4,128]{2,1,0:T(4,128)S(1)}, f32[2,4,128]{2,1,0:T(4,128)S(1)}, f32[2,4,128,128]{3,2,1,0:T(8,128)S(1)}, s32[8]{0:T(128)S(1)}, /...) while((s32[]{:T(128)}, f32[2,4,128]{2,1,0:T(4,128)S(1)}, ...), condition=%wide.region_6.7_spmd.clone, body=%wide.region_2.6_spmd.clone.sunk | while | flops 275925120 | bytes 9515759 | solution.py:122
  163.1 1.1 constant_dynamic-slice_fusion.3
  166.6 1.1 constant_dynamic-slice_fusion.3
  170.2 1.1 constant_dynamic-slice_fusion.3
  173.7 1.1 constant_dynamic-slice_fusion.3
  177.3 1.1 constant_dynamic-slice_fusion.3
  184.4 1.1 constant_dynamic-slice_fusion.3
  187.9 1.1 constant_dynamic-slice_fusion.3
  191.5 1.1 constant_dynamic-slice_fusion.3
  195.0 1.1 constant_dynamic-slice_fusion.3
  198.6 1.1 constant_dynamic-slice_fusion.3
  202.1 1.1 constant_dynamic-slice_fusion.3
  205.7 1.1 constant_dynamic-slice_fusion.3
  209.3 1.1 constant_dynamic-slice_fusion.3
  212.8 1.1 constant_dynamic-slice_fusion.3
  216.4 1.1 constant_dynamic-slice_fusion.3
  219.9 1.1 constant_dynamic-slice_fusion.3
  223.5 1.1 constant_dynamic-slice_fusion.3
  230.6 1.1 constant_dynamic-slice_fusion.3
  234.1 1.1 constant_dynamic-slice_fusion.3
  237.7 1.1 constant_dynamic-slice_fusion.3
  241.2 1.1 constant_dynamic-slice_fusion.3
  244.8 1.1 constant_dynamic-slice_fusion.3
  248.3 1.1 constant_dynamic-slice_fusion.3
  251.9 1.1 constant_dynamic-slice_fusion.3
  255.5 1.1 constant_dynamic-slice_fusion.3
  259.0 1.1 constant_dynamic-slice_fusion.3
  262.6 1.1 constant_dynamic-slice_fusion.3
  266.1 1.1 constant_dynamic-slice_fusion.3
  269.7 1.1 constant_dynamic-slice_fusion.3
  273.2 1.1 constant_dynamic-slice_fusion.3
  277.6 4.6 convolution_convert_fusion
  282.2 5.1 %all_to_all.16 = bf16[2,4,2048]{2,1,0:T(4,128)(2,1)S(1)} all-to-all(bf16[2,4,2048]{2,1,0:T(4,128)(2,1)S(1)} %bitcast.366), channel_id=1, replica_groups=mesh['ctx_0'=4,'ctx_1'=2,'ctx_2'=8,'ctx_3'=2,'head'=2] {'head'}, dimensions={0} | all-to-all | bytes 65536 | tf_op jit(solution)/shard_map/all_to_all | solution.py:33
  287.5 5.0 %all_to_all.17 = f32[2,1,4]{2,1,0:T(1,128)S(1)} all-to-all(f32[2,1,4]{2,1,0:T(1,128)S(1)} %broadcast_in_dim.94), channel_id=1, replica_groups=mesh['ctx_0'=4,'ctx_1'=2,'ctx_2'=8,'ctx_3'=2,'head'=2] {'head'}, dimensions={0} | all-to-all | bytes 64 | tf_op jit(solution)/shard_map/all_to_all | solution.py:39
  293.2 116.8 %all-gather.16.cloned.1.call-done = bf16[128,4,2048]{2,1,0:T(4,128)(2,1)} async-done(((bf16[1,4,2048]{2,1,0:T(4,128)(2,1)}), bf16[128,4,2048]{2,1,0:T(4,128)(2,1)}) %all-gather.16.cloned.1.call-update) | async-done | bytes 2097168 | tf_op jit(solution)/shard_map/all_gather | solution.py:183
  410.0 2.5 reshape.1099
  412.6 4.5 convolution_convert_fusion.1
  417.1 1.2 reshape.1077
  418.3 3.6 all-to-all-start.2
  421.9 13.2 %all-to-all-done.2 = bf16[2,512,501]{1,2,0:T(8,128)(2,1)S(1)} async-done(((bf16[2,512,501]{1,2,0:T(8,128)(2,1)}), bf16[2,512,501]{1,2,0:T(8,128)(2,1)S(1)}, u32[]{:S(2)}, u32[]{:S(2)}) %all-to-all-start.2) | async-done | bytes 1026080 | tf_op jit(solution)/shard_map/all_to_all | solution.py:33
  435.7 9.6 %all-gather.6 = f32[4,3,512]{2,1,0:T(4,128)S(1)} all-gather(f32[1,3,512]{2,1,0:T(4,128)S(1)} %maximum_bitcast_fusion), channel_id=2, replica_groups=mesh['ctx_0'=4,'ctx_1'=2,'ctx_2'=8,'ctx_3'=2,'head'=2] {'ctx_0'}, dimensions={0}, use_global_device_ids=true | all-gather | bytes 30720 | tf_op jit(solution)/shard_map/all_gather | solution.py:57
  445.3 4.7 all-gather.7
  450.1 18.4 %all-gather.8 = f32[8,3,512]{2,1,0:T(4,128)S(1)} all-gather(f32[1,3,512]{2,1,0:T(4,128)S(1)} %maximum_bitcast_fusion.2), channel_id=4, replica_groups=mesh['ctx_0'=4,'ctx_1'=2,'ctx_2'=8,'ctx_3'=2,'head'=2] {'ctx_2'}, dimensions={0}, use_global_device_ids=true | all-gather | bytes 55296 | tf_op jit(solution)/shard_map/all_gather | solution.py:57
  468.6 12.6 %all-gather.9 = f32[2,3,512]{2,1,0:T(4,128)S(1)} all-gather(f32[1,3,512]{2,1,0:T(4,128)S(1)} %maximum_bitcast_fusion.3), channel_id=5, replica_groups=mesh['ctx_0'=4,'ctx_1'=2,'ctx_2'=8,'ctx_3'=2,'head'=2] {'ctx_3'}, dimensions={0}, use_global_device_ids=true | all-gather | bytes 18432 | tf_op jit(solution)/shard_map/all_gather | solution.py:57
  481.2 3.2 all-gather.10
  (412 shorter events, 87.7 us)
Async XLA Ops:
  7.2 144.1 %all-gather.14.cloned.1.call-start = ((), (), s32[]{:S(2)}) async-start(), calls=%async_computation.3 | async-start | bytes 16908288 | tf_op jit(solution)/shard_map/all_gather | solution.py:19
  9.8 400.2 %all-gather.16.cloned.1.call-start = ((), (), s32[]{:S(2)}) async-start(), calls=%async_computation.4 | async-start | bytes 2113536 | tf_op jit(solution)/shard_map/all_gather | solution.py:183
  277.0 5.2 %copy-start = (bf16[128,1024]{1,0:T(8,128)(2,1)}, bf16[128,1024]{1,0:T(8,128)(2,1)S(1)}, u32[]{:S(2)}) copy-start(bf16[128,1024]{1,0:T(8,128)(2,1)S(1)} %convert_element_type.47) | copy-start | bytes 786436
  277.6 9.8 %copy-start.1 = (bf16[4,2048]{1,0:T(4,128)(2,1)S(1)}, bf16[4,2048]{1,0:T(4,128)(2,1)}, u32[]{:S(2)}) copy-start(bf16[4,2048]{1,0:T(4,128)(2,1)} %param.19) | copy-start | bytes 49156
  277.6 14.9 %copy-start.2 = (f32[2048]{0:T(1024)S(1)}, f32[2048]{0:T(1024)}, u32[]{:S(2)}) copy-start(f32[2048]{0:T(1024)} %param.20) | copy-start | bytes 24580
  417.1 4.8 copy-start.5
  418.3 16.8 %all-to-all-start.2 = ((bf16[2,512,501]{1,2,0:T(8,128)(2,1)}), bf16[2,512,501]{1,2,0:T(8,128)(2,1)S(1)}, u32[]{:S(2)}, u32[]{:S(2)}) async-start(bf16[2,512,501]{1,2,0:T(8,128)(2,1)} %bitcast.8), calls=%async_computation.2 | async-start | bytes 2064384 | tf_op jit(solution)/shard_map/all_to_all | solution.py:33
  421.9 62.6 %copy-start.3 = (f32[512]{0:T(512)S(1)}, f32[512]{0:T(512)}, u32[]{:S(2)}) copy-start(f32[512]{0:T(512)} %param.25) | copy-start | bytes 6148
  421.9 62.6 %copy-start.4 = (f32[512]{0:T(512)S(1)}, f32[512]{0:T(512)}, u32[]{:S(2)}) copy-start(f32[512]{0:T(512)} %param.24) | copy-start | bytes 6148
Sparse Core Ops, SparseCore 0:
  12.3 138.8 all-gather.13
  293.3 116.6 all-gather.15
where the time goes:
time: 493 us; the launch traced here: 492 us
  waiting for transfers between devices  268 us (54%)
  blocking collectives  58.6 us (12%)
  matrix products  56.6 us (11%)
  local copies, waits for them, and re-layouts  53.7 us (11%)
  other arithmetic  34.8 us (7%)
  between operations  14.4 us (3%)
    all_gather x1, waiting for transfers between devices, side_by_side(): whole, at, outs = (lax.all_gather(both, axis, axis=dim, tiled=True), 0, [])  138 us
    all_gather x1, waiting for transfers between devices, per_device(): lax.all_gather(normed, CTX, axis=0, tiled=True)  117 us
    all_gather x5, blocking collectives, all_in_one(): both, at, found = (lax.all_gather(jnp.concatenate(lines), axis), 0, {})  48.5 us
    dynamic_slice x32, local copies, waits for them, and re-layouts, one_block(): value_part = lax.dynamic_slice_in_dim(value_rows, start_row, block_rows, 0)  34.3 us
    dot_general x32, matrix products, attend_rows(): jnp.einsum('kgqr,rkd->kgqd', weights.astype(jnp.bfloat16), value_head_row...  30.3 us
    dot_general x32, matrix products, attend_rows(): jnp.einsum('qkgd,rkd->kgqr', query_heads, key_head_rows, preferred_elemen...  17.2 us
    reduce_sum x32, other arithmetic, attend_rows(): row_total = row_total * rescale + jnp.sum(weights, axis=-1)  16.7 us
    all_to_all x1, waiting for transfers between devices, sum_at_owner(): lax.all_to_all(pieces, axis, split_axis=0, concat_axis=0, tiled=True)  13.2 us
  transfers between devices with their start and end apart: 3, of which 3 were waited for; matrix products, arithmetic and copies ran while one was open for 1% of the time, Pallas kernels for 0%

commit v1 on v0

v1 whole, which is shorter than its diff:
```python
import functools

import jax
import jax.numpy as jnp
from jax import lax
from jax.experimental import pallas as pl
from jax.experimental.pallas import tpu as pltpu
from jax.sharding import Mesh
from jax.sharding import PartitionSpec as P

HEAD_SIZE = 128
GROUP = 4
DOCS = 8
AXES = ("ctx_0", "ctx_1", "ctx_2", "ctx_3", "head")
XYC = ("ctx_0", "ctx_1", "ctx_3")
XY = ("ctx_0", "ctx_1")
ZC = ("ctx_2", "ctx_3")
XYCH = ("ctx_0", "ctx_1", "ctx_3", "head")

LOG2E = 1.4426950408889634
SCORE_TO_LOG2 = HEAD_SIZE ** (-0.5) * LOG2E
MASKED = -1e30
NO_TOP = -1e20
KEY_BLOCK = 512


def size_of(axes):
    n = 1
    for a in axes:
        n *= lax.axis_size(a)
    return n


def spread(shard, axes):
    n = size_of(axes)
    return lax.all_to_all(
        jnp.broadcast_to(shard[None], (n, *shard.shape)), axes, 0, 0, tiled=True
    )


def swap_heads(shard):
    return lax.ppermute(shard, "head", [(0, 1), (1, 0)])


def attention_kernel(meta_ref, q_ref, kv_ref, out_ref, v_ref, m_ref, acc_ref):
    j = pl.program_id(0)
    keys = kv_ref.shape[0]
    rows = q_ref.shape[0] * q_ref.shape[1]

    @pl.when(j == 0)
    def _():
        v_ref[:, :HEAD_SIZE] = kv_ref[:, HEAD_SIZE:]
        v_ref[:, HEAD_SIZE:] = jnp.ones((keys, HEAD_SIZE), jnp.bfloat16)

    first_q = meta_ref[DOCS] + j * meta_ref[DOCS + 1]
    last_q = first_q + rows - 1
    first_k = meta_ref[DOCS + 2]

    def start_of(pos):
        low = jnp.int32(0)
        for d in range(DOCS):
            start = meta_ref[d]
            low = jnp.where(start <= pos, jnp.maximum(low, start), low)
        return low

    low_first = start_of(first_q)
    low_last = start_of(last_q)
    m_ref[...] = jnp.full(m_ref.shape, NO_TOP, jnp.float32)
    acc_ref[...] = jnp.zeros(acc_ref.shape, jnp.float32)
    block_lo = jnp.maximum(low_first - first_k, 0) // KEY_BLOCK
    block_hi = jnp.clip(last_q - first_k + KEY_BLOCK, 0, keys) // KEY_BLOCK

    def attend(b, masked):
        at = pl.multiple_of(b * KEY_BLOCK, KEY_BLOCK)
        k = kv_ref[pl.ds(at, KEY_BLOCK), :HEAD_SIZE]
        v = v_ref[pl.ds(at, KEY_BLOCK), :]
        if masked:
            pos = first_q + lax.broadcasted_iota(jnp.int32, (rows, 1), 0)
            low = jnp.zeros((rows, 1), jnp.int32)
            for d in range(DOCS):
                start = meta_ref[d]
                low = jnp.where(start <= pos, jnp.maximum(low, start), low)
            base = first_k + at
            key = lax.broadcasted_iota(jnp.int32, (rows, KEY_BLOCK), 1)
            allowed = (key >= low - base) & (key <= pos - base)
        for g in range(GROUP):
            q = q_ref[:, :, g * HEAD_SIZE : (g + 1) * HEAD_SIZE].reshape(rows, HEAD_SIZE)
            s = lax.dot_general(
                q, k, (((1,), (1,)), ((), ())), preferred_element_type=jnp.float32
            )
            if masked:
                s = jnp.where(allowed, s, MASKED)
            m_old = m_ref[g]
            m_new = jnp.maximum(
                m_old, jnp.max(s, axis=1, keepdims=True) * SCORE_TO_LOG2
            )
            p = jnp.exp2(s * SCORE_TO_LOG2 - m_new[:, :1]).astype(jnp.bfloat16)
            update = jnp.dot(p, v, preferred_element_type=jnp.float32)
            rescale = jnp.exp2(m_old - m_new)
            acc_ref[g] = acc_ref[g] * rescale[:, :1] + update
            m_ref[g] = m_new

    def step(b, carry):
        block_first = first_k + b * KEY_BLOCK
        free = (block_first >= low_last) & (block_first + KEY_BLOCK - 1 <= first_q)

        @pl.when(free)
        def _():
            attend(b, False)

        @pl.when(jnp.logical_not(free))
        def _():
            attend(b, True)

        return carry

    lax.fori_loop(block_lo, block_hi, step, 0)
    lane = lax.broadcasted_iota(jnp.int32, (rows, HEAD_SIZE), 1)
    stats = jnp.zeros((rows, HEAD_SIZE), jnp.float32)
    for g in range(GROUP):
        total = acc_ref[g][:, HEAD_SIZE:]
        some = total > 0.0
        total = jnp.where(some, total, 1.0)
        result = acc_ref[g][:, :HEAD_SIZE] / total
        out_ref[:, :, g * HEAD_SIZE : (g + 1) * HEAD_SIZE] = result.astype(
            jnp.bfloat16
        ).reshape(2, rows // 2, HEAD_SIZE)
        level = jnp.where(some, m_ref[g] + jnp.log2(total), NO_TOP)
        high = level.astype(jnp.bfloat16).astype(jnp.float32)
        rest = level - high
        middle = rest.astype(jnp.bfloat16).astype(jnp.float32)
        low = rest - middle
        stats = jnp.where(lane == g, high, stats)
        stats = jnp.where(lane == GROUP + g, middle, stats)
        stats = jnp.where(lane == 2 * GROUP + g, low, stats)
    out_ref[:, :, GROUP * HEAD_SIZE :] = stats.astype(jnp.bfloat16).reshape(
        2, rows // 2, HEAD_SIZE
    )


def partial_attention(meta, q_all, kv_all):
    blocks, half, width = q_all.shape
    keys = kv_all.shape[0]
    rows = 2 * half
    return pl.pallas_call(
        attention_kernel,
        grid_spec=pltpu.PrefetchScalarGridSpec(
            num_scalar_prefetch=1,
            grid=(blocks // 2,),
            in_specs=[
                pl.BlockSpec((2, half, width), lambda j, meta: (j, 0, 0)),
                pl.BlockSpec((keys, 2 * HEAD_SIZE), lambda j, meta: (0, 0)),
            ],
            out_specs=pl.BlockSpec((2, half, width + HEAD_SIZE), lambda j, meta: (j, 0, 0)),
            scratch_shapes=[
                pltpu.VMEM((keys, 2 * HEAD_SIZE), jnp.bfloat16),
                pltpu.VMEM((GROUP, rows, HEAD_SIZE), jnp.float32),
                pltpu.VMEM((GROUP, rows, 2 * HEAD_SIZE), jnp.float32),
            ],
        ),
        out_shape=jax.ShapeDtypeStruct((blocks, half, width + HEAD_SIZE), jnp.bfloat16),
        compiler_params=pltpu.CompilerParams(dimension_semantics=("arbitrary",)),
        name="partial_attention",
    )(meta, q_all, kv_all)


def merge_kernel(scored_ref, parts_ref, attended_ref, chosen_ref):
    windows = parts_ref.shape[0] // 2
    rows = parts_ref.shape[1]
    for c in range(2):
        levels = []
        for w in range(windows):
            st = parts_ref[2 * w + c, :, GROUP * HEAD_SIZE :].astype(jnp.float32)
            levels.append(
                st
                + pltpu.roll(st, HEAD_SIZE - GROUP, 1)
                + pltpu.roll(st, HEAD_SIZE - 2 * GROUP, 1)
            )
        top = functools.reduce(jnp.maximum, levels)
        shares = [jnp.exp2(level - top) for level in levels]
        total = functools.reduce(jnp.add, shares)
        shares = [share / total for share in shares]
        for g in range(GROUP):
            result = jnp.zeros((rows, HEAD_SIZE), jnp.float32)
            for w in range(windows):
                part = parts_ref[2 * w + c, :, g * HEAD_SIZE : (g + 1) * HEAD_SIZE]
                result = result + shares[w][:, g : g + 1] * part.astype(jnp.float32)
            at = (c * GROUP + g) * HEAD_SIZE
            attended_ref[:, at : at + HEAD_SIZE] = result.astype(jnp.bfloat16)
    count = scored_ref.shape[0]
    row = lax.broadcasted_iota(jnp.int32, (chosen_ref.shape[0], rows), 0)
    col = lax.broadcasted_iota(jnp.int32, (chosen_ref.shape[0], rows), 1)
    pick = jnp.zeros((chosen_ref.shape[0], rows), jnp.float32)
    for i in range(count):
        pick = jnp.where((row == i) & (col == scored_ref[i]), 1.0, pick)
    chosen_ref[...] = jnp.dot(
        pick.astype(jnp.bfloat16), attended_ref[...], preferred_element_type=jnp.float32
    ).astype(jnp.bfloat16)


def merged_attention(scored, parts):
    rows = parts.shape[1]
    width = 2 * GROUP * HEAD_SIZE
    return pl.pallas_call(
        merge_kernel,
        in_specs=[
            pl.BlockSpec(memory_space=pltpu.SMEM),
            pl.BlockSpec(memory_space=pltpu.VMEM),
        ],
        out_specs=(
            pl.BlockSpec(memory_space=pltpu.VMEM),
            pl.BlockSpec(memory_space=pltpu.VMEM),
        ),
        out_shape=(
            jax.ShapeDtypeStruct((rows, width), jnp.bfloat16),
            jax.ShapeDtypeStruct((16, width), jnp.bfloat16),
        ),
        name="merged_attention",
    )(scored, parts)


def merged_stats(stats, axis):
    tops, sums, targets = stats
    top = jnp.max(tops, axis=axis)
    total = jnp.sum(sums * jnp.exp(tops - jnp.expand_dims(top, axis)), axis=axis)
    return (top, total, jnp.sum(targets, axis=axis))


def per_device(
    queries,
    rotated_keys,
    value_matrix,
    doc_lengths,
    scored,
    residual,
    norm_gain,
    out_weight,
    lm_weight,
    token_ids,
    old_logp,
    advantage,
):
    tok_rows = queries.shape[0]
    count = scored.shape[0]
    cores = lax.axis_size("ctx_3")
    window_count = size_of(XY)
    z_count = lax.axis_size("ctx_2")
    window = lax.axis_index(XY)
    z = lax.axis_index("ctx_2")
    chip_rows = cores * tok_rows
    window_rows = z_count * chip_rows

    doc_starts = jnp.cumsum(doc_lengths) - doc_lengths
    meta = jnp.concatenate(
        [
            doc_starts.astype(jnp.int32),
            jnp.stack([z * chip_rows, jnp.int32(window_rows), window * window_rows]).astype(
                jnp.int32
            ),
        ]
    )
    by_core = jnp.swapaxes(queries.reshape(tok_rows, cores, GROUP * HEAD_SIZE), 0, 1)
    q_send = jnp.broadcast_to(by_core[None], (window_count, *by_core.shape)).reshape(
        window_count * cores, tok_rows, GROUP * HEAD_SIZE
    )
    kv = jnp.concatenate(
        [
            rotated_keys.reshape(tok_rows, cores, HEAD_SIZE),
            value_matrix.reshape(tok_rows, cores, HEAD_SIZE),
        ],
        axis=2,
    )
    kv = jnp.swapaxes(kv, 0, 1)
    kv_send = jnp.broadcast_to(kv[None], (z_count, *kv.shape)).reshape(
        z_count * cores, tok_rows, 2 * HEAD_SIZE
    )
    kv_all = lax.all_to_all(kv_send, ZC, 0, 0, tiled=True).reshape(-1, 2 * HEAD_SIZE)
    q_all = lax.all_to_all(q_send, XYC, 0, 0, tiled=True)
    parts = partial_attention(meta, q_all, kv_all)
    arrived = lax.all_to_all(parts, XYC, 0, 0, tiled=True)
    attended, chosen = merged_attention(scored, arrived)

    half = residual.shape[1]
    head = lax.axis_index("head")
    partial_value = jnp.dot(chosen, out_weight, preferred_element_type=jnp.float32)[:count]
    own = lax.dynamic_slice_in_dim(partial_value, head * half, half, 1)
    own = own + residual.astype(jnp.float32)
    partial_value = lax.dynamic_update_slice_in_dim(partial_value, own, head * half, 1)
    other = swap_heads(partial_value.astype(jnp.bfloat16)).astype(jnp.float32)
    hidden_all = partial_value + other
    squares = jnp.sum(hidden_all * hidden_all, axis=1, keepdims=True)
    hidden = own + lax.dynamic_slice_in_dim(other, head * half, half, 1)
    normed = (
        hidden * lax.rsqrt(squares / hidden_all.shape[1] + 1e-05) * norm_gain[None, :]
    ).astype(jnp.bfloat16)

    along_z = spread(normed, ("ctx_2",))
    along_xy = spread(along_z, XY)
    everyone = spread(along_xy, ("ctx_3",)).reshape(-1, half)
    row_count = everyone.shape[0]
    ids = token_ids.reshape(-1, cores, count).swapaxes(0, 1).reshape(row_count)
    partial_logits = jnp.dot(everyone, lm_weight, preferred_element_type=jnp.float32)
    rows = row_count // 2
    theirs = lax.dynamic_slice_in_dim(partial_logits, (1 - head) * rows, rows, 0)
    ours = lax.dynamic_slice_in_dim(partial_logits, head * rows, rows, 0)
    logits = ours + swap_heads(theirs.astype(jnp.bfloat16)).astype(jnp.float32)
    vocab_rows = logits.shape[1]
    my_index = (window * z_count + z) * cores + lax.axis_index("ctx_3")
    local_ids = lax.dynamic_slice_in_dim(ids, head * rows, rows, 0) - my_index * vocab_rows
    matches = local_ids[:, None] == jnp.arange(vocab_rows, dtype=jnp.int32)[None, :]
    target_part = jnp.sum(jnp.where(matches, logits, 0.0), axis=1)
    local_top = jnp.max(logits, axis=1)
    sum_part = jnp.sum(jnp.exp(logits - local_top[:, None]), axis=1)
    stats = jnp.stack([local_top, sum_part, target_part]).reshape(3, rows // 128, 128)
    by_z = spread(stats, ("ctx_2",))
    merged = merged_stats((by_z[:, 0], by_z[:, 1], by_z[:, 2]), 0)
    by_rest = spread(jnp.stack(merged), XYCH)
    by_rest = by_rest.reshape(-1, 2, 3, rows // 128, 128)
    top, total, target = merged_stats((by_rest[:, :, 0], by_rest[:, :, 1], by_rest[:, :, 2]), 0)
    log_probs = (target - top - jnp.log(total)).reshape(cores, row_count // (cores * count), count)
    log_probs = log_probs.swapaxes(0, 1).reshape(row_count)
    ratio = jnp.exp(jnp.clip(log_probs - old_logp, -4.0, 4.0))
    token_loss = -jnp.minimum(ratio * advantage, jnp.clip(ratio, 0.8, 1.2) * advantage)
    return (attended, log_probs, token_loss)


def solution(mesh):
    finer = Mesh(mesh.devices.reshape(4, 2, 8, 2, mesh.shape["head"]), AXES)
    ctx = AXES[:4]
    placed = (
        P(ctx, "head"),
        P(ctx, "head"),
        P(ctx, "head"),
        P(),
        P(ctx),
        P(ctx, "head"),
        P("head"),
        P("head", None),
        P("head", ctx),
        P(),
        P(),
        P(),
    )
    return jax.shard_map(
        per_device,
        mesh=finer,
        in_specs=placed,
        out_specs=(P(ctx, "head"), P(), P()),
        check_vma=False,
    )
```

time: 493 us -> 256 us (0.52)
  waiting for transfers between devices: 268 us -> 117 us
  starting transfers between devices: 3.66 us -> 51.2 us
  matrix products: 56.6 us -> 9.75 us
  local copies, waits for them, and re-layouts: 53.7 us -> 11.9 us
  other arithmetic: 34.8 us -> 2.55 us
  Pallas kernels: 0 us -> 17.4 us
  blocking collectives: 58.6 us -> 42.3 us
  between operations: 14.4 us -> 0.89 us
    all_gather x2 -> x0, waiting for transfers between devices: 255 us -> none  [the longest x1 138 us: side_by_side(): whole, at, outs = (lax.all_gather(both, axis, axis=dim, tiled=True), 0, [])]
    all_to_all x1 -> x4, waiting for transfers between devices: 13.2 us -> 103 us  [the longest x1 33.9 us: per_device(): arrived = lax.all_to_all(parts, XYC, 0, 0, tiled=True)]
    all_gather x5 -> x0, blocking collectives: 48.5 us -> none  [all_in_one(): both, at, found = (lax.all_gather(jnp.concatenate(lines), axis), 0, {})]
    dot_general x66 -> x2, matrix products: 56.6 us -> 9.75 us  [the longest x1 5.14 us: per_device(): jnp.dot(everyone, lm_weight, preferred_element_type=jnp.float32)]
    all_to_all x1 -> x4, starting transfers between devices: 3.58 us -> 50.2 us  [the longest x1 25.1 us: per_device(): arrived = lax.all_to_all(parts, XYC, 0, 0, tiled=True)]
    dynamic_slice x32 -> x0, local copies, waits for them, and re-layouts: 34.3 us -> none  [one_block(): value_part = lax.dynamic_slice_in_dim(value_rows, start_row, block_rows, 0)]
    all_to_all x2 -> x4, blocking collectives: 10.1 us -> 42.3 us  [spread(): lax.all_to_all(jnp.broadcast_to(shard[None], (n, *shard.shape)), axes, 0,...]
    reduce_sum x69 -> x5, other arithmetic: 19.9 us -> 0.26 us  [the longest x1 0.15 us: per_device(): squares = jnp.sum(hidden_all * hidden_all, axis=1, keepdims=True)]
  transfers between devices with their start and end apart: 3 -> 6, of which waited for: 3 -> 6; matrix products, arithmetic and copies ran while one was open for 1% -> 1% of each run, Pallas kernels for 0% -> 0%
where the time goes in v1:
time: 256 us; the launch traced here: 253 us
  waiting for transfers between devices  117 us (46%)
  starting transfers between devices  51.2 us (20%)
  blocking collectives  42.3 us (17%)
  Pallas kernels  17.4 us (7%)
  local copies, waits for them, and re-layouts  11.9 us (5%)
  matrix products  9.75 us (4%)
    all_to_all x4, blocking collectives, spread(): lax.all_to_all(jnp.broadcast_to(shard[None], (n, *shard.shape)), axes, 0,...  42.3 us
    all_to_all x1, waiting for transfers between devices, per_device(): arrived = lax.all_to_all(parts, XYC, 0, 0, tiled=True)  33.9 us
    all_to_all x1, waiting for transfers between devices, per_device(): q_all = lax.all_to_all(q_send, XYC, 0, 0, tiled=True)  28.1 us
    all_to_all x1, waiting for transfers between devices, per_device(): lax.all_to_all(kv_send, ZC, 0, 0, tiled=True).reshape(-1, 2 * HEAD_SIZE)  27.2 us
    all_to_all x1, starting transfers between devices, per_device(): arrived = lax.all_to_all(parts, XYC, 0, 0, tiled=True)  25.1 us
    ppermute x2, waiting for transfers between devices, swap_heads(): return lax.ppermute(shard, 'head', [(0, 1), (1, 0)])  14.6 us
    all_to_all x1, waiting for transfers between devices, spread(): lax.all_to_all(jnp.broadcast_to(shard[None], (n, *shard.shape)), axes, 0,...  13.7 us
    pallas_call x1, Pallas kernels, partial_attention(): pl.pallas_call(attention_kernel, grid_spec=pltpu.PrefetchScalarGridSpec(n...  12.8 us
  transfers between devices with their start and end apart: 6, of which 6 were waited for; matrix products, arithmetic and copies ran while one was open for 1% of the time, Pallas kernels for 0%

profile of v1, /device:TPU:1, one launch (start us, length us, event | category | flops | bytes accessed | tf_op | source)
XLA Modules:
  0.0 253.4 jit_solution(5889805679711588808)
XLA Ops:
  0.6 1.1 reshape.99
  1.8 1.6 broadcast_in_dim.19
  3.4 8.6 %all-to-all-start = ((bf16[16,128,512]{2,1,0:T(8,128)(2,1)}), bf16[16,128,512]{2,1,0:T(8,128)(2,1)S(1)}, u32[]{:S(2)}, u32[]{:S(2)}) async-start(bf16[16,128,512]{2,1,0:T(8,128)(2,1)} %bitcast.52), calls=%async_computation | async-start | bytes 4194304 | tf_op jit(solution)/shard_map/all_to_all | solution.py:278
  12.0 0.0 copy-start.11
  12.0 0.1 maximum_bitcast_fusion
  12.2 28.1 %all-to-all-done.q_ref = bf16[16,128,512]{2,1,0:T(8,128)(2,1)S(1)} async-done(((bf16[16,128,512]{2,1,0:T(8,128)(2,1)}), bf16[16,128,512]{2,1,0:T(8,128)(2,1)S(1)}, u32[]{:S(2)}, u32[]{:S(2)}) %all-to-all-start) | async-done | bytes 2097184 | tf_op jit(solution)/shard_map/all_to_all | solution.py:278
  40.3 1.2 broadcast_in_dim.20
  41.4 9.4 %all-to-all-start.1 = ((bf16[16,128,256]{2,1,0:T(8,128)(2,1)}), bf16[16,128,256]{2,1,0:T(8,128)(2,1)S(1)}, u32[]{:S(2)}, u32[]{:S(2)}) async-start(bf16[16,128,256]{2,1,0:T(8,128)(2,1)} %bitcast.7), calls=%async_computation.1 | async-start | bytes 2097152 | tf_op jit(solution)/shard_map/all_to_all | solution.py:277
  50.9 0.2 reduce-window.9
  51.1 0.6 pad_add_fusion.meta_ref
  51.7 27.2 %all-to-all-done.1 = bf16[16,128,256]{2,1,0:T(8,128)(2,1)S(1)} async-done(((bf16[16,128,256]{2,1,0:T(8,128)(2,1)}), bf16[16,128,256]{2,1,0:T(8,128)(2,1)S(1)}, u32[]{:S(2)}, u32[]{:S(2)}) %all-to-all-start.1) | async-done | bytes 1048608 | tf_op jit(solution)/shard_map/all_to_all | solution.py:277
  78.9 1.0 copy-done.2
  79.9 12.8 %partial_attention.1 = bf16[16,128,640]{2,1,0:T(8,128)(2,1)} custom-call(s32[11]{0:T(128)} %pad_add_fusion.meta_ref, bf16[16,128,512]{2,1,0:T(8,128)(2,1)} %copy-done.1, bf16[2048,256]{1,0:T(8,128)(2,1)} %bitcast.53), custom_call_target="tpu_custom_call" | custom-call | tf_op jit(solution)/shard_map/partial_attention/pallas_call | solution.py:145
  92.7 25.1 %all-to-all-start.2 = ((bf16[16,128,640]{2,1,0:T(8,128)(2,1)}), bf16[16,128,640]{2,1,0:T(8,128)(2,1)S(1)}, u32[]{:S(2)}, u32[]{:S(2)}) async-start(bf16[16,128,640]{2,1,0:T(8,128)(2,1)} %partial_attention.1), calls=%async_computation.2 | async-start | bytes 5242880 | tf_op jit(solution)/shard_map/all_to_all | solution.py:280
  117.7 33.9 %all-to-all-done.2.parts_ref = bf16[16,128,640]{2,1,0:T(8,128)(2,1)S(1)} async-done(((bf16[16,128,640]{2,1,0:T(8,128)(2,1)}), bf16[16,128,640]{2,1,0:T(8,128)(2,1)S(1)}, u32[]{:S(2)}, u32[]{:S(2)}) %all-to-all-start.2) | async-done | bytes 2621472 | tf_op jit(solution)/shard_map/all_to_all | solution.py:280
  151.7 1.5 copy-done
  153.2 4.6 %merged_attention.1 = (bf16[128,1024]{1,0:T(8,128)(2,1)}, bf16[16,1024]{1,0:T(8,128)(2,1)}) custom-call(s32[4]{0:T(128)} %scored_ref.1, bf16[16,128,640]{2,1,0:T(8,128)(2,1)} %copy-done), custom_call_target="tpu_custom_call" | custom-call | tf_op jit(solution)/shard_map/merged_attention/pallas_call | solution.py:204
  157.8 4.6 %fusion.7 = f32[4,4096]{1,0:T(4,128)S(1)} fusion(bf16[1024,4096]{1,0:T(8,128)(2,1)} %param.19, bf16[16,1024]{1,0:T(8,128)(2,1)} %get-tuple-element.6), kind=kOutput, calls=%fused_computation.22 | convolution fusion | flops 33554432 | bytes 8462336 | tf_op jit(solution)/shard_map/dot_general | solution.py:285
  162.4 0.0 copy-done.5
  162.5 0.5 collective-permute-start
  162.9 2.4 collective-permute-done
  165.3 0.1 multiply_reduce_fusion
  165.5 0.1 multiply_convert_fusion
  165.6 11.1 %all_to_all.40 = bf16[8,4,2048]{2,1,0:T(4,128)(2,1)S(1)} all-to-all(bf16[8,4,2048]{2,1,0:T(4,128)(2,1)S(1)} %broadcast_in_dim.21), channel_id=1, replica_groups=mesh['ctx_0'=4,'ctx_1'=2,'ctx_2'=8,'ctx_3'=2,'head'=2] {'ctx_2'}, dimensions={0} | all-to-all | bytes 262144 | tf_op jit(solution)/shard_map/all_to_all | solution.py:36
  176.7 1.5 broadcast_in_dim.22
  178.2 7.1 %all-to-all-start.4 = ((bf16[8,8,4,2048]{3,2,1,0:T(4,128)(2,1)}), bf16[8,8,4,2048]{3,2,1,0:T(4,128)(2,1)S(1)}, u32[]{:S(2)}, u32[]{:S(2)}) async-start(bf16[8,8,4,2048]{3,2,1,0:T(4,128)(2,1)} %broadcast_in_dim.22), calls=%async_computation.4 | async-start | bytes 2097152 | tf_op jit(solution)/shard_map/all_to_all | solution.py:36
  185.3 13.7 %all-to-all-done.4 = bf16[8,8,4,2048]{3,2,1,0:T(4,128)(2,1)S(1)} async-done(((bf16[8,8,4,2048]{3,2,1,0:T(4,128)(2,1)}), bf16[8,8,4,2048]{3,2,1,0:T(4,128)(2,1)S(1)}, u32[]{:S(2)}, u32[]{:S(2)}) %all-to-all-start.4) | async-done | bytes 1048608 | tf_op jit(solution)/shard_map/all_to_all | solution.py:36
  199.0 1.1 broadcast_in_dim.23
  200.1 8.6 %all_to_all.41 = bf16[2,8,8,4,2048]{4,3,2,1,0:T(4,128)(2,1)S(1)} all-to-all(bf16[2,8,8,4,2048]{4,3,2,1,0:T(4,128)(2,1)S(1)} %broadcast_in_dim.23), channel_id=1, replica_groups=mesh['ctx_0'=4,'ctx_1'=2,'ctx_2'=8,'ctx_3'=2,'head'=2] {'ctx_3'}, dimensions={0} | all-to-all | bytes 4194304 | tf_op jit(solution)/shard_map/all_to_all | solution.py:36
  208.7 2.1 reshape.105
  210.8 5.1 %fusion.11 = f32[512,1002]{0,1:T(8,128)S(1)} fusion(bf16[512,2048]{1,0:T(8,128)(2,1)} %reshape.105, bf16[2048,1002]{0,1:T(8,128)(2,1)} %param.20), kind=kOutput, calls=%fused_computation.37 | convolution fusion | flops 2101346304 | bytes 8253440 | tf_op jit(solution)/shard_map/dot_general | solution.py:302
  215.9 0.1 dynamic-slice_convert_fusion
  216.0 0.5 collective-permute-start.1
  216.5 0.1 reshape.106
  216.7 0.1 reshape.107
  216.8 0.0 copy-start.9
  216.8 0.0 copy-start.10
  216.8 0.1 dynamic-slice_subtract_fusion
  216.9 12.2 %collective-permute-done.1 = bf16[256,1002]{0,1:T(8,128)(2,1)S(1)} collective-permute-done((bf16[256,1002]{0,1:T(8,128)(2,1)S(1)}, bf16[256,1002]{0,1:T(8,128)(2,1)S(1)}, u32[]{:S(2)}, u32[]{:S(2)}) %collective-permute-start.1) | collective-permute-done | bytes 513056 | tf_op jit(solution)/shard_map/ppermute | solution.py:42
  229.1 0.2 fusion
  229.3 0.4 exponential_reduce_fusion
  229.6 9.1 %all_to_all.42 = f32[8,3,2,128]{3,2,1,0:T(2,128)S(1)} all-to-all(f32[8,3,2,128]{3,2,1,0:T(2,128)S(1)} %broadcast_in_dim.27), channel_id=1, replica_groups=mesh['ctx_0'=4,'ctx_1'=2,'ctx_2'=8,'ctx_3'=2,'head'=2] {'ctx_2'}, dimensions={0} | all-to-all | bytes 49152 | tf_op jit(solution)/shard_map/all_to_all | solution.py:36
  238.9 13.4 %all_to_all.43 = f32[32,3,2,128]{3,2,1,0:T(2,128)S(1)} all-to-all(f32[32,3,2,128]{3,2,1,0:T(2,128)S(1)} %broadcast_in_dim.28), channel_id=1, replica_groups=mesh['ctx_0'=4,'ctx_1'=2,'ctx_2'=8,'ctx_3'=2,'head'=2] {'ctx_0','ctx_1',..., dimensions={0} | all-to-all | bytes 196608 | tf_op jit(solution)/shard_map/all_to_all | solution.py:36
  252.4 0.1 sub.63
  252.6 0.1 copy.51
  252.6 0.1 reshape.109
  252.8 0.0 copy-start.6
  252.8 0.6 minimum_negate_fusion
  (40 shorter events, 0.4 us)
Async XLA Ops:
  3.4 8.6 %copy-start.3 = (bf16[128,256]{1,0:T(8,128)(2,1)S(1)}, bf16[128,256]{1,0:T(8,128)(2,1)}, u32[]{:S(2)}) copy-start(bf16[128,256]{1,0:T(8,128)(2,1)} %param.14) | copy-start | bytes 196612
  3.4 8.6 %copy-start.4 = (bf16[128,256]{1,0:T(8,128)(2,1)S(1)}, bf16[128,256]{1,0:T(8,128)(2,1)}, u32[]{:S(2)}) copy-start(bf16[128,256]{1,0:T(8,128)(2,1)} %param.13) | copy-start | bytes 196612
  3.4 36.9 %all-to-all-start = ((bf16[16,128,512]{2,1,0:T(8,128)(2,1)}), bf16[16,128,512]{2,1,0:T(8,128)(2,1)S(1)}, u32[]{:S(2)}, u32[]{:S(2)}) async-start(bf16[16,128,512]{2,1,0:T(8,128)(2,1)} %bitcast.52), calls=%async_computation | async-start | bytes 4194304 | tf_op jit(solution)/shard_map/all_to_all | solution.py:278
  12.0 38.9 %copy-start.11 = (s32[8]{0:T(128)S(1)}, s32[8]{0:T(128)}, u32[]{:S(2)}) copy-start(s32[8]{0:T(128)} %param.15) | copy-start | bytes 100
  40.3 38.6 %copy-start.1 = (bf16[16,128,512]{2,1,0:T(8,128)(2,1)}, bf16[16,128,512]{2,1,0:T(8,128)(2,1)S(1)}, u32[]{:S(2)}) copy-start(bf16[16,128,512]{2,1,0:T(8,128)(2,1)S(1)} %all-to-all-done.q_ref) | copy-start | bytes 6291460
  41.4 37.4 %all-to-all-start.1 = ((bf16[16,128,256]{2,1,0:T(8,128)(2,1)}), bf16[16,128,256]{2,1,0:T(8,128)(2,1)S(1)}, u32[]{:S(2)}, u32[]{:S(2)}) async-start(bf16[16,128,256]{2,1,0:T(8,128)(2,1)} %bitcast.7), calls=%async_computation.1 | async-start | bytes 2097152 | tf_op jit(solution)/shard_map/all_to_all | solution.py:277
  78.9 1.0 copy-start.2
  92.7 59.0 %all-to-all-start.2 = ((bf16[16,128,640]{2,1,0:T(8,128)(2,1)}), bf16[16,128,640]{2,1,0:T(8,128)(2,1)S(1)}, u32[]{:S(2)}, u32[]{:S(2)}) async-start(bf16[16,128,640]{2,1,0:T(8,128)(2,1)} %partial_attention.1), calls=%async_computation.2 | async-start | bytes 5242880 | tf_op jit(solution)/shard_map/all_to_all | solution.py:280
  151.7 1.5 copy-start
  157.8 4.6 %copy-start.5 = (bf16[4,2048]{1,0:T(4,128)(2,1)S(1)}, bf16[4,2048]{1,0:T(4,128)(2,1)}, u32[]{:S(2)}) copy-start(bf16[4,2048]{1,0:T(4,128)(2,1)} %param.17) | copy-start | bytes 49156
  157.8 7.7 %copy-start.7 = (f32[2048]{0:T(1024)S(1)}, f32[2048]{0:T(1024)}, u32[]{:S(2)}) copy-start(f32[2048]{0:T(1024)} %param.18) | copy-start | bytes 24580
  162.5 2.9 %collective-permute-start = (bf16[4,4096]{1,0:T(4,128)(2,1)S(1)}, bf16[4,4096]{1,0:T(4,128)(2,1)S(1)}, u32[]{:S(2)}, u32[]{:S(2)}) collective-permute-start(bf16[4,4096]{1,0:T(4,128)(2,1)S(1)} %convert_element_type.19), channel_id=1, source_target_pairs={{0,1},{1,0},{2,3},{3,2},{4,5},{5,4},{6,7},{7,6},{8,9},{9,8},{10,11... | collective-permute-start | bytes 98312 | tf_op jit(solution)/shard_map/ppermute | solution.py:42
  178.2 20.8 %all-to-all-start.4 = ((bf16[8,8,4,2048]{3,2,1,0:T(4,128)(2,1)}), bf16[8,8,4,2048]{3,2,1,0:T(4,128)(2,1)S(1)}, u32[]{:S(2)}, u32[]{:S(2)}) async-start(bf16[8,8,4,2048]{3,2,1,0:T(4,128)(2,1)} %broadcast_in_dim.22), calls=%async_computation.4 | async-start | bytes 2097152 | tf_op jit(solution)/shard_map/all_to_all | solution.py:36
  210.8 5.7 %copy-start.8 = (s32[512]{0:T(512)S(1)}, s32[512]{0:T(512)}, u32[]{:S(2)}) copy-start(s32[512]{0:T(512)} %param.21) | copy-start | bytes 6148
  216.0 13.1 %collective-permute-start.1 = (bf16[256,1002]{0,1:T(8,128)(2,1)S(1)}, bf16[256,1002]{0,1:T(8,128)(2,1)S(1)}, u32[]{:S(2)}, u32[]{:S(2)}) collective-permute-start(bf16[256,1002]{0,1:T(8,128)(2,1)S(1)} %dynamic-slice_convert_fusion), channel_id=1, source_target_pairs={{0,1},{1,0},{2,3},{3,2},{4,5},{5,4},{6,7},{7,6},{8,9},{9,8},{10,11... | collective-permute-start | bytes 1539080 | tf_op jit(solution)/shard_map/ppermute | solution.py:42
  216.8 36.0 %copy-start.9 = (f32[512]{0:T(512)S(1)}, f32[512]{0:T(512)}, u32[]{:S(2)}) copy-start(f32[512]{0:T(512)} %param.23) | copy-start | bytes 6148
  216.8 35.9 %copy-start.10 = (f32[512]{0:T(512)S(1)}, f32[512]{0:T(512)}, u32[]{:S(2)}) copy-start(f32[512]{0:T(512)} %param.22) | copy-start | bytes 6148
  252.8 0.6 copy-start.6
